TPU v7x, 32 devices: a whole 2x2x4 slice. The times are simulated.
32 devices in a mesh: dp: 4 (over y, core), mp: 8 (over z, x).
Axes of the slice: x: 2, y: 2, z: 4, core: 2. Of those that a mesh axis runs over, the one named last changes fastest.
Arguments:
- table: bfloat16 [16384, 1024], P('mp'), may hold values from -200 to 200
- triples: int32 [32, 3], P('dp'), may hold values from 0 to 16383
- words: int32 [32, 61], P('dp'), may hold values from 0 to 16383
- labels: int32 [32], P('dp'), may hold values 0 or 1
- in_gain: float32 [1024], replicated, may hold values from 0.5 to 1.5
- up_weight: bfloat16 [1024, 4096], P(None, 'mp'), may hold values from -0.1875 to 0.1875
- down_weight: bfloat16 [4096, 1024], P('mp'), may hold values from -0.09375 to 0.09375
- out_gain: float32 [1024], P('mp'), may hold values from 0.5 to 1.5
- class_weight: float32 [1024], P('mp'), may hold values from -6 to 6
Outputs:
- encoded: bfloat16 [2048, 1024], P('dp', 'mp')
- scores: float32 [32], P('dp')
- class_grad: float32 [1024], P('mp')
All inputs are finite; a program needn't handle non-finite values. No bound on the sum of `labels` on one device may be relied on, other than what follows from the above.
Results may differ from a plain program's by a relative error of at most 0.0075.
Values may be sent and summed in bfloat16 or wider, within the bound.
A program may use at most 64 MiB of HBM per device.

v0:
```python
import jax
import jax.numpy as jnp
from jax import lax
from jax.sharding import PartitionSpec as P


def normalize(values, first, second, width, gain):
    mean = first / width
    var = second / width - mean * mean
    return (values - mean[:, None]) * lax.rsqrt(var + 1e-05)[:, None] * gain


def own_rows(table, ids, place):
    entries = table.shape[0]
    local = ids - place * entries
    inside = (local >= 0) & (local < entries)
    picked = jnp.take(table, jnp.clip(local, 0, entries - 1), axis=0).astype(jnp.float32)
    return jnp.where(inside[:, None], picked, 0.0)


def on_device(
    table, triples, words, labels, in_gain, up_weight, down_weight, out_gain, class_weight
):
    ids = jnp.concatenate([triples, words], axis=1).reshape(-1)
    seq_len = triples.shape[1] + words.shape[1]
    tok_rows = ids.shape[0]
    width = table.shape[1]
    share = width // lax.axis_size("mp")
    place = lax.axis_index("mp")
    embed = lax.psum_scatter(own_rows(table, ids, place), "mp", scatter_dimension=1, tiled=True)
    first, second = lax.psum((jnp.sum(embed, axis=1), jnp.sum(embed * embed, axis=1)), "mp")
    gain_cols = lax.dynamic_slice_in_dim(in_gain, place * share, share, 0)
    own = normalize(embed, first, second, width, gain_cols).astype(jnp.bfloat16)
    hidden = jnp.dot(
        lax.all_gather(own, "mp", axis=1, tiled=True), up_weight, preferred_element_type=jnp.float32
    )
    active = jax.nn.gelu(hidden, approximate=False).astype(jnp.bfloat16)
    terms = jnp.dot(active, down_weight, preferred_element_type=jnp.float32)
    mixed = lax.psum_scatter(terms, "mp", scatter_dimension=1, tiled=True)
    resid = own.astype(jnp.float32) + mixed
    first_out, second_out = lax.psum((jnp.sum(resid, axis=1), jnp.sum(resid * resid, axis=1)), "mp")
    encoded = normalize(resid, first_out, second_out, width, out_gain).astype(jnp.bfloat16)
    pooled = jnp.mean(
        encoded.astype(jnp.float32).reshape(tok_rows // seq_len, seq_len, share), axis=1
    )
    partial_score = jnp.dot(pooled, class_weight, precision=lax.Precision.HIGHEST)
    scores = lax.psum(partial_score, "mp")
    diff = jax.nn.sigmoid(scores) - labels.astype(jnp.float32)
    class_grad = lax.psum(jnp.dot(diff, pooled, precision=lax.Precision.HIGHEST), "dp")
    return (encoded, scores, class_grad)


def solution(mesh):
    return jax.shard_map(
        on_device,
        mesh=mesh,
        in_specs=(
            P("mp", None),
            P("dp", None),
            P("dp", None),
            P("dp"),
            P(),
            P(None, "mp"),
            P("mp", None),
            P("mp"),
            P("mp"),
        ),
        out_specs=(P("dp", "mp"), P("dp"), P("mp")),
        check_vma=False,
    )
```

profile of v0, /device:TPU:0, one launch (start us, length us, event | category | flops | bytes accessed | tf_op | source)
XLA Modules:
  0.0 274.6 jit_solution(6279800719337923860)
XLA Ops:
  7.2 0.0 copy-start
  7.2 0.0 reduce-scatter.3.cloned.1.call-start
  7.2 0.8 copy.12
  8.1 0.8 compare_and_fusion
  8.8 0.8 broadcast_clamp_fusion
  9.6 0.1 min.18
  9.7 0.1 min.16
  9.7 0.1 and.19
  9.9 5.5 %gather_fusion = bf16[512,1024]{1,0:T(8,128)(2,1)S(1)} fusion(bf16[2048,1024]{1,0:T(8,128)(2,1)} %param.9, s32[1024]{0:T(1024)S(1)} %pad_clamp_fusion), kind=kCustom, calls=%fused_computation | custom fusion | bytes 2099200 | tf_op jit(solution)/shard_map/jit(_take)/gather | solution.py:17
  15.3 1.7 convert_select_fusion
  17.0 0.0 reduce-scatter.3.cloned.1.call-update
  17.0 0.0 all-gather.2.cloned.1.call-start
  17.1 0.8 dynamic_slice.3
  17.9 71.1 %reduce-scatter.3.cloned.1.call-done = f32[512,128]{1,0:T(8,128)} async-done(((f32[512,1024]{1,0:T(8,128)}), f32[512,128]{1,0:T(8,128)}) %reduce-scatter.3.cloned.1.call-update) | async-done | bytes 262160 | tf_op jit(solution)/shard_map/reduce_scatter | solution.py:30
  89.0 1.2 fusion.86
  90.2 19.2 %all-reduce.1 = (f32[512]{0:T(512)S(1)}, f32[512]{0:T(512)S(1)}) all-reduce(f32[512]{0:T(512)S(1)} %get-tuple-element.6, f32[512]{0:T(512)S(1)} %get-tuple-element.5), channel_id=1, replica_groups=mesh['dp'=4,'mp'=8] {'mp'}, use_global_device_ids=true, to_apply=%region_4.5 | all-reduce | flops 1024 | bytes 8192 | tf_op jit(solution)/shard_map/psum | solution.py:31
  109.4 1.8 multiply_convert_fusion.1
  111.2 0.0 all-gather.2.cloned.1.call-update
  111.2 0.0 reduce-scatter.5.cloned.1.call-start
  111.3 36.8 %all-gather.2.cloned.1.call-done = bf16[512,1024]{1,0:T(8,128)(2,1)} async-done(((bf16[512,128]{1,0:T(8,128)(2,1)}), bf16[512,1024]{1,0:T(8,128)(2,1)}) %all-gather.2.cloned.1.call-update) | async-done | bytes 1048592 | tf_op jit(solution)/shard_map/all_gather | solution.py:35
  148.0 0.0 copy-done
  148.0 0.0 copy-done.4
  148.0 6.0 %fusion.10 = f32[512,1024]{1,0:T(8,128)} fusion(bf16[512,1024]{1,0:T(8,128)(2,1)S(1)} %copy-done, bf16[512,1024]{1,0:T(8,128)(2,1)} %all-gather.2.cloned.1.call-done, bf16[1024,512]{1,0:T(8,128)(2,1)S(1)} %copy-done.4), kind=kOutput, calls=%fused_computation.23 | convolution fusion | flops 1090781184 | bytes 5242880 | tf_op jit(solution)/shard_map/dot_general | solution.py:38
  154.0 0.0 reduce-scatter.5.cloned.1.call-update
  154.0 68.0 %reduce-scatter.5.cloned.1.call-done = f32[512,128]{1,0:T(8,128)} async-done(((f32[512,1024]{1,0:T(8,128)}), f32[512,128]{1,0:T(8,128)}) %reduce-scatter.5.cloned.1.call-update) | async-done | bytes 262160 | tf_op jit(solution)/shard_map/reduce_scatter | solution.py:39
  222.0 1.3 fusion.42
  223.4 19.2 %all-reduce = (f32[512]{0:T(512)S(1)}, f32[512]{0:T(512)S(1)}) all-reduce(f32[512]{0:T(512)S(1)} %get-tuple-element.4, f32[512]{0:T(512)S(1)} %get-tuple-element.3), channel_id=1, replica_groups=mesh['dp'=4,'mp'=8] {'mp'}, use_global_device_ids=true, to_apply=%region_9.10 | all-reduce | flops 1024 | bytes 8192 | tf_op jit(solution)/shard_map/psum | solution.py:41
  242.5 2.0 convert_reduce_fusion
  244.5 0.1 convolution_bitcast_fusion.1
  244.6 17.1 %psum.46 = f32[8]{0:T(128)S(1)} all-reduce(f32[8]{0:T(128)S(1)} %convolution_bitcast_fusion.1), channel_id=1, replica_groups=mesh['dp'=4,'mp'=8] {'mp'}, use_global_device_ids=true, to_apply=%region_11.12 | all-reduce | flops 8 | bytes 64 | tf_op jit(solution)/shard_map/psum | solution.py:47
  261.7 0.1 convolution_bitcast_fusion
  261.9 6.1 %psum.47 = f32[128]{0:T(128)} all-reduce(f32[128]{0:T(128)S(1)} %convolution_bitcast_fusion), channel_id=1, replica_groups=mesh['dp'=4,'mp'=8] {'dp'}, use_global_device_ids=true, to_apply=%region_12.13 | all-reduce | flops 128 | bytes 1024 | tf_op jit(solution)/shard_map/psum | solution.py:49
  (16 shorter events, 0.1 us)
Async XLA Ops:
  7.2 140.8 %copy-start = (bf16[512,1024]{1,0:T(8,128)(2,1)S(1)}, bf16[512,1024]{1,0:T(8,128)(2,1)}, u32[]{:S(2)}) copy-start(bf16[512,1024]{1,0:T(8,128)(2,1)} %param.15) | copy-start | bytes 3145732
  7.2 81.9 %reduce-scatter.3.cloned.1.call-start = ((), (), s32[]{:S(2)}) async-start(), calls=%async_computation.2 | async-start | bytes 2359296 | tf_op jit(solution)/shard_map/reduce_scatter | solution.py:30
  17.0 131.0 %copy-start.4 = (bf16[1024,512]{1,0:T(8,128)(2,1)S(1)}, bf16[1024,512]{1,0:T(8,128)(2,1)}, u32[]{:S(2)}) copy-start(bf16[1024,512]{1,0:T(8,128)(2,1)} %param.14) | copy-start | bytes 3145732
  17.0 131.0 %all-gather.2.cloned.1.call-start = ((), (), s32[]{:S(2)}) async-start(), calls=%async_computation.3 | async-start | bytes 1179648 | tf_op jit(solution)/shard_map/all_gather | solution.py:35
  111.2 110.8 %reduce-scatter.5.cloned.1.call-start = ((), (), s32[]{:S(2)}) async-start(), calls=%async_computation.4 | async-start | bytes 2359296 | tf_op jit(solution)/shard_map/reduce_scatter | solution.py:39
  154.0 68.1 %copy-start.1 = (f32[512,128]{1,0:T(8,128)S(1)}, f32[512,128]{1,0:T(8,128)}, u32[]{:S(2)}) copy-start(f32[512,128]{1,0:T(8,128)} %reduce-scatter.3.cloned.1.call-done) | copy-start | bytes 786436
  154.0 88.6 %copy-start.3 = (f32[128]{0:T(128)S(1)}, f32[128]{0:T(128)}, u32[]{:S(2)}) copy-start(f32[128]{0:T(128)} %param.16) | copy-start | bytes 1540
  154.0 90.5 %copy-start.2 = (f32[128]{0:T(128)S(1)}, f32[128]{0:T(128)}, u32[]{:S(2)}) copy-start(f32[128]{0:T(128)} %param.17) | copy-start | bytes 1540
  154.0 107.8 %copy-start.5 = (s32[8]{0:T(128)S(1)}, s32[8]{0:T(128)}, u32[]{:S(2)}) copy-start(s32[8]{0:T(128)} %param.12) | copy-start | bytes 100
  261.7 6.3 %copy-start.6 = (f32[8]{0:T(128)}, f32[8]{0:T(128)S(1)}, u32[]{:S(2)}) copy-start(f32[8]{0:T(128)S(1)} %psum.46) | copy-start | bytes 100
Sparse Core Ops, SparseCore 0:
  17.1 71.8 reduce-scatter.2
  111.3 36.6 all-gather.1
  154.1 67.8 reduce-scatter.4
where the time goes:
time: 275 us
  waiting for transfers between devices  176 us (64%)
  blocking collectives  61.6 us (22%)
  between operations  13.8 us (5%)
  other arithmetic  9.47 us (3%)
  local copies, waits for them, and re-layouts  7.4 us (3%)
  matrix products  6.22 us (2%)
    reduce_scatter x1, waiting for transfers between devices, on_device(): lax.psum_scatter(own_rows(table, ids, place), 'mp', scatter_dimension=1,...  71.1 us
    reduce_scatter x1, waiting for transfers between devices, on_device(): mixed = lax.psum_scatter(terms, 'mp', scatter_dimension=1, tiled=True)  68 us
    all_gather x1, waiting for transfers between devices, on_device(): lax.all_gather(own, 'mp', axis=1, tiled=True)  36.8 us
    psum x1, blocking collectives, on_device(): lax.psum((jnp.sum(resid, axis=1), jnp.sum(resid * resid, axis=1)), 'mp')  19.2 us
    psum x1, blocking collectives, on_device(): lax.psum((jnp.sum(embed, axis=1), jnp.sum(embed * embed, axis=1)), 'mp')  19.2 us
    psum x1, blocking collectives, on_device(): scores = lax.psum(partial_score, 'mp')  17.1 us
    psum x1, blocking collectives, on_device(): lax.psum(jnp.dot(diff, pooled, precision=lax.Precision.HIGHEST), 'dp')  6.15 us
    dot_general x1, matrix products, on_device(): terms = jnp.dot(active, down_weight, preferred_element_type=jnp.float32)  5.96 us
  transfers between devices with their start and end apart: 3, of which 3 were waited for; matrix products, arithmetic and copies ran while one was open for 0% of the time, Pallas kernels for 0%

commit v1 on v0

v1 whole, which is shorter than its diff:
```python
import functools
import math

import jax
import jax.numpy as jnp
from jax import lax
from jax.experimental import pallas as pl
from jax.experimental.pallas import tpu as pltpu
from jax.sharding import PartitionSpec as P

MESH = pl.DeviceIdType.MESH
BF16 = jnp.bfloat16
F32 = jnp.float32


def each(count, body):
    if count <= 8:
        for k in range(count):
            body(k)
    else:
        lax.fori_loop(0, count, lambda k, c: (body(k), c)[1], 0)


def norm_rows(values, gain, width):
    mean = jnp.sum(values, axis=1, keepdims=True) / width
    var = jnp.sum(values * values, axis=1, keepdims=True) / width - mean * mean
    return ((values - mean) * lax.rsqrt(var + 1e-05) * gain).astype(BF16)


def kernel(
    n, ndp, seq,
    ids, table, up, down, in_gain, out_gain, class_w, labels,
    enc_out, score_out, grad_out,
    tab_v, up_v, down_v, a_send, a_recv, b_send, b_recv, gath, c_send, c_recv, part,
    d_send, d_recv, og_all, cw_all, e_send, e_recv, s_send, s_recv, q_send, q_recv,
    loc_sem, a_ss, a_rs, b_ss, b_rs, gz_ss, gx_ss, g_rs, c_ss, c_rs, d_ss, d_rs,
    w_ss, w_rs, e_ss, e_rs, s_ss, s_rs, q_ss, q_rs,
):
    Z = n // 2
    me = lax.axis_index("mp")
    dme = lax.axis_index("dp")
    z, x = me // 2, me % 2
    ox = 1 - x
    partner = z * 2 + ox
    tok = ids.shape[1]
    width = table.shape[1]
    entries = table.shape[0]
    feat = enc_out.shape[2]
    triples = labels.shape[0]

    def remote(src, dst, ss, rs, mp=None, dp=None):
        where = {"mp": mp} if dp is None else {"dp": dp}
        return pltpu.make_async_remote_copy(
            src_ref=src, dst_ref=dst, send_sem=ss, recv_sem=rs, device_id=where, device_id_type=MESH
        )

    loads = [
        pltpu.make_async_copy(src, dst, loc_sem.at[i])
        for i, (src, dst) in enumerate(((table, tab_v), (up, up_v), (down, down_v)))
    ]
    for copy in loads:
        copy.start()

    barrier = pltpu.get_barrier_semaphore()

    def greet(j):
        pl.semaphore_signal(barrier, inc=1, device_id={"mp": (me + 1 + j) % n}, device_id_type=MESH)

    each(n - 1, greet)
    for j in range(1, ndp):
        pl.semaphore_signal(barrier, inc=1, device_id={"dp": (dme + j) % ndp}, device_id_type=MESH)

    loads[0].wait()

    def half(side):
        local = jnp.concatenate([ids[zk * 2 + side] for zk in range(Z)], axis=0) - me * entries
        lanes = lax.broadcasted_iota(jnp.int32, (local.shape[0], entries), 1)
        hot = jnp.where(lanes == local, 1.0, 0.0).astype(BF16)
        embed = jnp.dot(hot, tab_v[...], preferred_element_type=F32)
        return norm_rows(embed, in_gain[...], width)

    rows = half(ox)
    for zk in range(Z):
        a_send[zk] = rows[zk * tok:(zk + 1) * tok]
    pl.semaphore_wait(barrier, n - 1 + ndp - 1)

    def a_copy(zk):
        return remote(a_send.at[zk], a_recv.at[zk], a_ss.at[zk], a_rs.at[zk], mp=partner)

    each(Z, lambda k: a_copy((z + 1 + k) % Z).start())

    def w_copies(j):
        p = (me + 1 + j) % n
        return (
            remote(out_gain, og_all.at[me], w_ss.at[0, p], w_rs.at[0, me], mp=p),
            remote(class_w, cw_all.at[me], w_ss.at[1, p], w_rs.at[1, me], mp=p),
        )

    def w_start(j):
        for copy in w_copies(j):
            copy.start()

    each(n - 1, w_start)
    og_all[me] = out_gain[...]
    cw_all[me] = class_w[...]

    rows = half(x)
    for zk in range(Z):
        b_send[zk] = rows[zk * tok:(zk + 1) * tok]

    def b_copy(zk):
        return remote(b_send.at[zk], b_recv.at[z], b_ss.at[zk], b_rs.at[z], mp=zk * 2 + x)

    def b_step(k):
        zk = (z + 1 + k) % Z
        a_copy(zk).wait_recv()
        b_send[zk] = b_send[zk] + a_recv[zk]
        if isinstance(k, int) and k == Z - 1:
            return
        b_copy(zk).start()

    each(Z - 1, b_step)
    b_step(Z - 1)

    def from_z(k):
        return (z + Z - 1 - k) % Z

    def b_in(zs):
        return remote(b_send.at[z], b_recv.at[zs], b_ss.at[z], b_rs.at[zs], mp=me)

    each(Z - 1, lambda k: b_in(from_z(k)).wait_recv())
    total = b_send[z]
    if Z <= 8:
        for k in range(Z - 1):
            total = total + b_recv[from_z(k)]
    else:
        total = lax.fori_loop(0, Z - 1, lambda k, t: t + b_recv[from_z(k)], total)
    gath[me] = total

    def gz_copy(zk):
        return remote(gath.at[me], gath.at[me], gz_ss.at[zk], g_rs.at[me], mp=zk * 2 + x)

    def gx_copy(zk):
        b = zk * 2 + x
        return remote(gath.at[b], gath.at[b], gx_ss.at[zk], g_rs.at[b], mp=partner)

    def g_in(b):
        return remote(gath.at[b], gath.at[b], gz_ss.at[z], g_rs.at[b], mp=me)

    gx_copy(z).start()
    each(Z - 1, lambda k: gz_copy((z + 1 + k) % Z).start())
    loads[1].wait()
    loads[2].wait()

    def c_copy(zk):
        return remote(c_send.at[zk], c_recv.at[zk], c_ss.at[zk], c_rs.at[zk], mp=partner)

    def d_copy(zk):
        return remote(d_send.at[zk], d_recv.at[z], d_ss.at[zk], d_rs.at[z], mp=zk * 2 + x)

    def ffn(zs, own):
        if not own:
            g_in(zs * 2 + x).wait_recv()
            gx_copy(zs).start()
        g_in(zs * 2 + ox).wait_recv()
        both = jnp.concatenate([gath[zs * 2 + ox], gath[zs * 2 + x]], axis=0)
        hidden = jnp.dot(both, up_v[...], preferred_element_type=F32)
        active = (0.5 * hidden * (1.0 + lax.erf(hidden * (1.0 / math.sqrt(2.0))))).astype(BF16)
        terms = jnp.dot(active, down_v[...], preferred_element_type=F32)
        c_send[zs] = terms[:tok].astype(BF16)
        c_copy(zs).start()
        part[zs] = terms[tok:]

    def pass_on(zs):
        c_copy(zs).wait_recv()
        d_send[zs] = (part[zs] + c_recv[zs].astype(F32)).astype(BF16)
        d_copy(zs).start()

    ffn(z, True)

    def step(k):
        ffn(from_z(k), False)
        if isinstance(k, int):
            if k > 0:
                pass_on(from_z(k - 1))
        else:
            pl.when(k > 0)(lambda: pass_on(from_z(k - 1)))

    each(Z - 1, step)
    pass_on(from_z(Z - 2))

    c_copy(z).wait_recv()
    mixed = part[z] + c_recv[z].astype(F32)

    def d_in(zs):
        return remote(d_send.at[z], d_recv.at[zs], d_ss.at[z], d_rs.at[zs], mp=me)

    each(Z - 1, lambda k: d_in(from_z(k)).wait_recv())
    if Z <= 8:
        for k in range(Z - 1):
            mixed = mixed + d_recv[from_z(k)].astype(F32)
    else:
        mixed = lax.fori_loop(0, Z - 1, lambda k, t: t + d_recv[from_z(k)].astype(F32), mixed)
    resid = gath[me].astype(F32) + mixed

    def w_in(j):
        src = (me + n - 1 - j) % n
        for i, (ref, dst) in enumerate(((out_gain, og_all), (class_w, cw_all))):
            remote(ref, dst.at[src], w_ss.at[i, me], w_rs.at[i, src], mp=me).wait_recv()

    each(n - 1, w_in)
    gain = jnp.concatenate([og_all[p] for p in range(n)], axis=1)
    weight = jnp.concatenate([cw_all[p] for p in range(n)], axis=1)
    encoded = norm_rows(resid, gain, width)
    for p in range(n):
        e_send[p] = encoded[:, p * feat:(p + 1) * feat]
    score = jnp.sum(encoded.astype(F32) * weight) / seq
    s_send[...] = jnp.full(s_send.shape, score, F32)

    def e_copies(j):
        p = (me + 1 + j) % n
        return (
            remote(e_send.at[p], e_recv.at[me], e_ss.at[p], e_rs.at[me], mp=p),
            remote(s_send, s_recv.at[me], s_ss.at[p], s_rs.at[me], mp=p),
        )

    def e_start(j):
        for copy in e_copies(j):
            copy.start()

    each(n - 1, e_start)
    e_recv[me] = e_send[me]
    s_recv[me] = s_send[...]

    def e_in(j):
        src = (me + n - 1 - j) % n
        remote(e_send.at[me], e_recv.at[src], e_ss.at[me], e_rs.at[src], mp=me).wait_recv()
        remote(s_send, s_recv.at[src], s_ss.at[me], s_rs.at[src], mp=me).wait_recv()

    each(n - 1, e_in)
    per = n // triples
    lane = lax.broadcasted_iota(jnp.int32, (1, triples), 1)
    scores = jnp.zeros((1, triples), F32)
    grad = jnp.zeros((1, feat), F32)
    for t in range(triples):
        logit = s_recv[t * per]
        block = jnp.sum(e_recv[t * per].astype(F32), axis=0, keepdims=True)
        for p in range(t * per + 1, (t + 1) * per):
            logit = logit + s_recv[p]
            block = block + jnp.sum(e_recv[p].astype(F32), axis=0, keepdims=True)
        scores = jnp.where(lane == t, logit[0:1, :triples], scores)
        diff = jax.nn.sigmoid(logit[0:1, :feat]) - labels[t].astype(F32)
        grad = grad + diff * (block / seq)
    q_send[...] = grad

    def q_copy(j):
        return remote(
            q_send, q_recv.at[dme], q_ss.at[j], q_rs.at[dme], dp=(dme + j) % ndp
        )

    for j in range(1, ndp):
        q_copy(j).start()
    score_out[...] = scores
    enc_out[...] = e_recv[...]

    each(Z, lambda k: a_copy((z + 1 + k) % Z).wait_send())
    each(Z - 1, lambda k: b_copy((z + 1 + k) % Z).wait_send())
    each(Z - 1, lambda k: gz_copy((z + 1 + k) % Z).wait_send())
    each(Z, lambda k: gx_copy((z + 1 + k) % Z).wait_send())
    each(Z, lambda k: c_copy((z + 1 + k) % Z).wait_send())
    each(Z - 1, lambda k: d_copy((z + 1 + k) % Z).wait_send())

    def ends(j):
        for copy in w_copies(j) + e_copies(j):
            copy.wait_send()

    each(n - 1, ends)
    for j in range(1, ndp):
        src = (dme + ndp - j) % ndp
        remote(q_send, q_recv.at[src], q_ss.at[j], q_rs.at[src], dp=dme).wait_recv()
        grad = grad + q_recv[src]
        q_copy(j).wait_send()
    grad_out[...] = grad


def on_device(
    n, ndp, table, triples, words, labels, in_gain, up_weight, down_weight, out_gain, class_weight
):
    ids = jnp.concatenate([triples, words], axis=1)
    seq = ids.shape[1]
    rows = ids.size
    tok = rows // n
    entries, width = table.shape
    units = up_weight.shape[1]
    feat = width // n
    Z = n // 2
    T = triples.shape[0]
    dma = pltpu.SemaphoreType.DMA
    vm = pl.BlockSpec(memory_space=pltpu.VMEM)
    hbm = pl.BlockSpec(memory_space=pl.ANY)
    zblk = pltpu.VMEM((Z, tok, width), BF16)
    wide = max(128, feat)
    enc, scores, grad = pl.pallas_call(
        functools.partial(kernel, n, ndp, seq),
        out_shape=(
            jax.ShapeDtypeStruct((n, tok, feat), BF16),
            jax.ShapeDtypeStruct((1, T), F32),
            jax.ShapeDtypeStruct((1, feat), F32),
        ),
        in_specs=[vm, hbm, hbm, hbm, vm, vm, vm, pl.BlockSpec(memory_space=pltpu.SMEM)],
        out_specs=(vm, vm, vm),
        scratch_shapes=[
            pltpu.VMEM((entries, width), BF16),
            pltpu.VMEM((width, units), BF16),
            pltpu.VMEM((units, width), BF16),
            zblk, zblk, zblk, zblk,
            pltpu.VMEM((n, tok, width), BF16),
            zblk, zblk,
            pltpu.VMEM((Z, tok, width), F32),
            zblk, zblk,
            pltpu.VMEM((n, 1, feat), F32),
            pltpu.VMEM((n, 1, feat), F32),
            pltpu.VMEM((n, tok, feat), BF16),
            pltpu.VMEM((n, tok, feat), BF16),
            pltpu.VMEM((8, wide), F32),
            pltpu.VMEM((n, 8, wide), F32),
            pltpu.VMEM((1, feat), F32),
            pltpu.VMEM((ndp, 1, feat), F32),
            dma((3,)),
            dma((Z,)), dma((Z,)), dma((Z,)), dma((Z,)),
            dma((Z,)), dma((Z,)), dma((n,)),
            dma((Z,)), dma((Z,)), dma((Z,)), dma((Z,)),
            dma((2, n)), dma((2, n)),
            dma((n,)), dma((n,)), dma((n,)), dma((n,)),
            dma((ndp,)), dma((ndp,)),
        ],
        compiler_params=pltpu.CompilerParams(
            collective_id=0, has_side_effects=True, vmem_limit_bytes=48 * 1024 * 1024
        ),
    )(
        ids.reshape(n, tok, 1), table, up_weight, down_weight, in_gain.reshape(1, -1),
        out_gain.reshape(1, -1), class_weight.reshape(1, -1), labels,
    )
    return enc.reshape(rows, feat), scores.reshape(-1), grad.reshape(-1)


def solution(mesh):
    return jax.shard_map(
        functools.partial(on_device, mesh.shape["mp"], mesh.shape["dp"]),
        mesh=mesh,
        in_specs=(
            P("mp", None), P("dp", None), P("dp", None), P("dp"), P(),
            P(None, "mp"), P("mp", None), P("mp"), P("mp"),
        ),
        out_specs=(P("dp", "mp"), P("dp"), P("mp")),
        check_vma=False,
    )
```

time: 275 us -> 81.2 us (0.30)
  waiting for transfers between devices: 176 us -> 0 us
  Pallas kernels: 0 us -> 71.8 us
  blocking collectives: 61.6 us -> 0 us
  between operations: 13.8 us -> 0.66 us
  other arithmetic: 9.47 us -> 0.76 us
  matrix products: 6.22 us -> 0 us
    reduce_scatter x2 -> x0, waiting for transfers between devices: 139 us -> none  [the longest x1 71.1 us: on_device(): lax.psum_scatter(own_rows(table, ids, place), 'mp', scatter_dimension=1,...]
    pallas_call x0 -> x1, Pallas kernels: none -> 71.8 us  [on_device(): pl.pallas_call(functools.partial(kernel, n, ndp, seq), out_shape=(jax.Sha...]
    psum x4 -> x0, blocking collectives: 61.6 us -> none  [the longest x1 19.2 us: on_device(): lax.psum((jnp.sum(resid, axis=1), jnp.sum(resid * resid, axis=1)), 'mp')]
    all_gather x1 -> x0, waiting for transfers between devices: 36.8 us -> none  [on_device(): lax.all_gather(own, 'mp', axis=1, tiled=True)]
    unnamed x15 -> x16, local copies, waits for them, and re-layouts: 0.87 us -> 7.54 us
    dot_general x3 -> x0, matrix products: 6.22 us -> none  [the longest x1 5.96 us: on_device(): terms = jnp.dot(active, down_weight, preferred_element_type=jnp.float32)]
    gather x1 -> x0, local copies, waits for them, and re-layouts: 5.46 us -> none  [own_rows(): jnp.take(table, jnp.clip(local, 0, entries - 1), axis=0).astype(jnp.float32)]
    reduce_sum x3 -> x0, other arithmetic: 4.43 us -> none  [the longest x1 1.95 us: on_device(): jnp.mean(encoded.astype(jnp.float32).reshape(tok_rows // seq_len, seq_len...]
  transfers between devices with their start and end apart: 3 -> 0, of which waited for: 3 -> 0; matrix products, arithmetic and copies ran while one was open for 0% -> 0% of each run, Pallas kernels for 0% -> 0%
where the time goes in v1:
time: 81.2 us; the launch traced here: 80.9 us
  Pallas kernels  71.8 us (88%)
  local copies, waits for them, and re-layouts  7.69 us (9%)
    pallas_call x1, Pallas kernels, on_device(): pl.pallas_call(functools.partial(kernel, n, ndp, seq), out_shape=(jax.Sha...  71.8 us
    unnamed x16, local copies, waits for them, and re-layouts  7.54 us

profile of v1, /device:TPU:0, one launch (start us, length us, event | category | flops | bytes accessed | tf_op | source)
XLA Modules:
  0.0 80.9 jit_solution(12512799460253032185)
XLA Ops:
  0.6 0.8 copy.13
  1.4 0.8 add_bitcast_fusion
  2.1 0.1 copy.14.ids
  2.3 0.0 copy-start
  2.3 1.2 %copy-done = bf16[1024,512]{1,0:T(8,128)(2,1)S(1)} copy-done((bf16[1024,512]{1,0:T(8,128)(2,1)S(1)}, bf16[1024,512]{1,0:T(8,128)(2,1)}, u32[]{:S(2)}) %copy-start) | copy-done | bytes 1048600
  3.5 0.0 copy-start.1
  3.5 1.2 %copy-done.1 = bf16[512,1024]{1,0:T(8,128)(2,1)S(1)} copy-done((bf16[512,1024]{1,0:T(8,128)(2,1)S(1)}, bf16[512,1024]{1,0:T(8,128)(2,1)}, u32[]{:S(2)}) %copy-start.1) | copy-done | bytes 1048600
  4.8 0.0 copy-start.2
  4.8 0.7 copy-done.2
  5.5 0.0 copy-start.3
  5.5 0.7 copy-done.3
  6.1 0.0 copy-start.4
  6.1 0.7 copy-done.4
  6.8 0.0 copy-start.5
  6.8 0.7 copy-done.5
  7.4 71.8 %shard_map.112 = (bf16[8,64,128]{2,1,0:T(8,128)(2,1)S(1)}, f32[1,8]{1,0:T(1,128)S(1)}, f32[1,128]{1,0:T(1,128)S(1)}) custom-call(s32[8,64,1]{2,1,0:T(8,128)S(1)} %copy.14.ids, bf16[2048,1024]{1,0:T(8,128)(2,1)} %table.1, bf16[1024,512]{1,0:T(8,128)(2,1)S(1)} %copy-done, bf16[512,1024]{1,0:T(8,128)(2,1)S(1)} %copy-done.1, f32[1,1024]{1,0:T(1,128)S(1)} %bitcast.9, ...), custom_call_target="tpu_custom_call" | custom-call | tf_op jit(solution)/shard_map/pallas_call | solution.py:303
  79.2 0.7 copy.18
  79.9 0.5 copy.19
  80.4 0.5 copy.20
Async XLA Ops:
  2.3 1.2 %copy-start = (bf16[1024,512]{1,0:T(8,128)(2,1)S(1)}, bf16[1024,512]{1,0:T(8,128)(2,1)}, u32[]{:S(2)}) copy-start(bf16[1024,512]{1,0:T(8,128)(2,1)} %up.1) | copy-start | bytes 3145732
  3.5 1.2 %copy-start.1 = (bf16[512,1024]{1,0:T(8,128)(2,1)S(1)}, bf16[512,1024]{1,0:T(8,128)(2,1)}, u32[]{:S(2)}) copy-start(bf16[512,1024]{1,0:T(8,128)(2,1)} %down.1) | copy-start | bytes 3145732
  4.8 0.7 copy-start.2
  5.5 0.7 copy-start.3
  6.1 0.7 copy-start.4
  6.8 0.7 copy-start.5

commit v2 on v1

v2 whole, which is shorter than its diff:
```python
import functools
import math

import jax
import jax.numpy as jnp
from jax import lax
from jax.experimental import pallas as pl
from jax.experimental.pallas import tpu as pltpu
from jax.sharding import PartitionSpec as P

MESH = pl.DeviceIdType.MESH
BF16 = jnp.bfloat16
F32 = jnp.float32


def each(count, body):
    if count <= 8:
        for k in range(count):
            body(k)
    else:
        lax.fori_loop(0, count, lambda k, c: (body(k), c)[1], 0)


def norm_rows(values, gain, width):
    mean = jnp.sum(values, axis=1, keepdims=True) / width
    var = jnp.sum(values * values, axis=1, keepdims=True) / width - mean * mean
    return ((values - mean) * lax.rsqrt(var + 1e-05) * gain).astype(BF16)


def kernel(
    n, ndp, seq,
    ids, table, up, down, in_gain, out_gain, class_w, labels,
    enc_out, score_out, grad_out,
    tab_v, up_v, down_v, upx_v, downx_v, a_send, a_recv, own, sw_send, sw_recv,
    rows_v, terms_v, keep, part, d_send, d_recv,
    og_all, cw_all, e_send, e_recv, s_send, s_recv, q_send, q_recv,
    loc_sem, wx_ss, wx_rs, wy_ss, wy_rs, wc_ss, wc_rs, a_ss, a_rs, sw_ss, sw_rs, d_ss, d_rs,
    w_ss, w_rs, e_ss, e_rs, s_ss, s_rs, q_ss, q_rs,
):
    Z = n // 2
    me = lax.axis_index("mp")
    dme = lax.axis_index("dp")
    z, x = me // 2, me % 2
    ox = 1 - x
    partner = z * 2 + ox
    across = (dme + ndp // 2) % ndp
    beside = dme // 2 * 2 + 1 - dme % 2
    chunks, chunk_rows, width = own.shape
    r = chunk_rows // Z
    entries = table.shape[0]
    units = up.shape[1]
    feat = enc_out.shape[2]
    triples = labels.shape[0]

    def remote(src, dst, ss, rs, mp=None, dp=None):
        where = {"mp": mp} if dp is None else {"dp": dp}
        return pltpu.make_async_remote_copy(
            src_ref=src, dst_ref=dst, send_sem=ss, recv_sem=rs, device_id=where, device_id_type=MESH
        )

    loads = [
        pltpu.make_async_copy(src, dst, loc_sem.at[i])
        for i, (src, dst) in enumerate(((table, tab_v), (up, up_v), (down, down_v)))
    ]
    for copy in loads:
        copy.start()

    barrier = pltpu.get_barrier_semaphore()

    def greet(j):
        pl.semaphore_signal(barrier, inc=1, device_id={"mp": (me + 1 + j) % n}, device_id_type=MESH)

    each(n - 1, greet)
    for j in range(1, ndp):
        pl.semaphore_signal(barrier, inc=1, device_id={"dp": (dme + j) % ndp}, device_id_type=MESH)
    pl.semaphore_wait(barrier, n - 1 + ndp - 1)

    def quarter(ref, d):
        size = ref.shape[0] // ndp
        return ref.at[pl.ds(pl.multiple_of(d * size, size), size)]

    pairs = ((up, upx_v), (down, downx_v))

    def wx_copy(i):
        src, dst = pairs[i]
        return remote(quarter(src, dme), quarter(dst, dme), wx_ss.at[i], wx_rs.at[i], mp=partner)

    def wy_copy(i, d):
        ref = pairs[i][1]
        return remote(quarter(ref, d), quarter(ref, d), wy_ss.at[i], wy_rs.at[i], dp=across)

    def wc_copy(i, d, k):
        ref = pairs[i][1]
        return remote(quarter(ref, d), quarter(ref, d), wc_ss.at[i, k], wc_rs.at[i, k], dp=beside)

    wx_copy(0).start()
    wx_copy(1).start()

    def w_copies(j):
        p = (me + 1 + j) % n
        return (
            remote(out_gain, og_all.at[me], w_ss.at[0, p], w_rs.at[0, me], mp=p),
            remote(class_w, cw_all.at[me], w_ss.at[1, p], w_rs.at[1, me], mp=p),
        )

    def w_start(j):
        for copy in w_copies(j):
            copy.start()

    each(n - 1, w_start)
    og_all[me] = out_gain[...]
    cw_all[me] = class_w[...]
    loads[0].wait()

    def half(side):
        local = ids[side] - me * entries
        lanes = lax.broadcasted_iota(jnp.int32, (local.shape[0], entries), 1)
        hot = jnp.where(lanes == local, 1.0, 0.0).astype(BF16)
        embed = jnp.dot(hot, tab_v[...], preferred_element_type=F32)
        return norm_rows(embed, in_gain[...], width)

    def a_copy(j):
        return remote(a_send.at[j], a_recv.at[j], a_ss.at[j], a_rs.at[j], mp=partner)

    rows = half(ox)
    for j in range(chunks):
        a_send[j] = rows[j * chunk_rows:(j + 1) * chunk_rows]
        a_copy(j).start()
    rows = half(x)
    for j in range(chunks):
        own[j] = rows[j * chunk_rows:(j + 1) * chunk_rows]

    for i in range(2):
        wx_copy(i).wait_recv()
        wy_copy(i, dme).start()
        wc_copy(i, dme, 0).start()

    first = z // (Z // 2)
    second = 1 - first
    edge = jnp.logical_or(z == 0, z == Z - 1)
    inner = jnp.logical_not(edge)

    def sweep(way, j):
        return remote(
            sw_send.at[way, j], sw_recv.at[way, j], sw_ss.at[way, j], sw_rs.at[way, j],
            mp=(z + 1 - 2 * way) * 2 + x,
        )

    def sweep_in(way, j):
        return remote(
            sw_send.at[way, j], sw_recv.at[way, j], sw_ss.at[way, j], sw_rs.at[way, j], mp=me
        )

    def arrive(j):
        a_copy(j).wait_recv()
        own[j] = own[j] + a_recv[j]

        @pl.when(edge)
        def _():
            sw_recv[first, j] = jnp.zeros((chunk_rows, width), BF16)

        @pl.when(inner)
        def _():
            sweep_in(first, j).wait_recv()

        sw_send[first, j] = own[j] + sw_recv[first, j]
        sweep(first, j).start()

    def d_copy(j, zk):
        return remote(
            d_send.at[j, zk], d_recv.at[j, z], d_ss.at[j, zk], d_rs.at[j, z], mp=zk * 2 + x
        )

    def act(hidden):
        return (0.5 * hidden * (1.0 + lax.erf(hidden * (1.0 / math.sqrt(2.0))))).astype(BF16)

    def finish(j):
        sweep_in(second, j).wait_recv()

        @pl.when(inner)
        def _():
            sw_send[second, j] = own[j] + sw_recv[second, j]
            sweep(second, j).start()

        full = own[j] + sw_recv[0, j] + sw_recv[1, j]
        for zk in range(Z):
            rows_v[zk] = full[zk * r:(zk + 1) * r]
        keep[j] = rows_v[z].astype(F32)
        if j == 0:
            for i in range(2):
                wc_copy(i, beside, 0).wait_recv()
                wc_copy(i, (beside + ndp // 2) % ndp, 1).wait_recv()
            loads[1].wait()
            loads[2].wait()
        mine = act(jnp.dot(full, up_v[...], preferred_element_type=F32))
        theirs = act(jnp.dot(full, upx_v[...], preferred_element_type=F32))
        terms = jnp.dot(mine, down_v[...], preferred_element_type=F32)
        terms = terms + jnp.dot(theirs, downx_v[...], preferred_element_type=F32)
        for zk in range(Z):
            terms_v[zk] = terms[zk * r:(zk + 1) * r]
            d_send[j, zk] = terms[zk * r:(zk + 1) * r].astype(BF16)
        each(Z - 1, lambda k: d_copy(j, (z + 1 + k) % Z).start())
        part[j] = terms_v[z]

    lag = min(2, chunks)
    for t in range(chunks + lag):
        if t < chunks:
            arrive(t)
        if t == 0:
            for i in range(2):
                wy_copy(i, across).wait_recv()
                wc_copy(i, across, 1).start()
        if t >= lag:
            finish(t - lag)

    def w_in(j):
        src = (me + n - 1 - j) % n
        for i, (ref, dst) in enumerate(((out_gain, og_all), (class_w, cw_all))):
            remote(ref, dst.at[src], w_ss.at[i, me], w_rs.at[i, src], mp=me).wait_recv()

    each(n - 1, w_in)
    gain = jnp.concatenate([og_all[p] for p in range(n)], axis=1)
    weight = jnp.concatenate([cw_all[p] for p in range(n)], axis=1)

    def d_in(j, zs):
        return remote(d_send.at[j, z], d_recv.at[j, zs], d_ss.at[j, z], d_rs.at[j, zs], mp=me)

    score = jnp.zeros((), F32)
    for j in range(chunks):
        each(Z - 1, lambda k: d_in(j, (z + 1 + k) % Z).wait_recv())
        resid = keep[j] + part[j]
        if Z <= 8:
            for k in range(Z - 1):
                resid = resid + d_recv[j, (z + 1 + k) % Z].astype(F32)
        else:
            resid = lax.fori_loop(
                0, Z - 1, lambda k, t: t + d_recv[j, (z + 1 + k) % Z].astype(F32), resid
            )
        encoded = norm_rows(resid, gain, width)
        for p in range(n):
            e_send[p, j * r:(j + 1) * r] = encoded[:, p * feat:(p + 1) * feat]
        score = score + jnp.sum(encoded.astype(F32) * weight)
    s_send[...] = jnp.full(s_send.shape, score / seq, F32)

    def e_copies(j):
        p = (me + 1 + j) % n
        return (
            remote(e_send.at[p], e_recv.at[me], e_ss.at[p], e_rs.at[me], mp=p),
            remote(s_send, s_recv.at[me], s_ss.at[p], s_rs.at[me], mp=p),
        )

    def e_start(j):
        for copy in e_copies(j):
            copy.start()

    each(n - 1, e_start)
    e_recv[me] = e_send[me]
    s_recv[me] = s_send[...]

    def e_in(j):
        src = (me + n - 1 - j) % n
        remote(e_send.at[me], e_recv.at[src], e_ss.at[me], e_rs.at[src], mp=me).wait_recv()
        remote(s_send, s_recv.at[src], s_ss.at[me], s_rs.at[src], mp=me).wait_recv()

    each(n - 1, e_in)
    per = n // triples
    lane = lax.broadcasted_iota(jnp.int32, (1, triples), 1)
    scores = jnp.zeros((1, triples), F32)
    grad = jnp.zeros((1, feat), F32)
    for t in range(triples):
        logit = s_recv[t * per]
        block = jnp.sum(e_recv[t * per].astype(F32), axis=0, keepdims=True)
        for p in range(t * per + 1, (t + 1) * per):
            logit = logit + s_recv[p]
            block = block + jnp.sum(e_recv[p].astype(F32), axis=0, keepdims=True)
        scores = jnp.where(lane == t, logit[0:1, :triples], scores)
        diff = jax.nn.sigmoid(logit[0:1, :feat]) - labels[t].astype(F32)
        grad = grad + diff * (block / seq)
    q_send[...] = grad

    def q_copy(j):
        return remote(
            q_send, q_recv.at[dme], q_ss.at[j], q_rs.at[dme], dp=(dme + j) % ndp
        )

    for j in range(1, ndp):
        q_copy(j).start()
    score_out[...] = scores
    enc_out[...] = e_recv[...]

    for j in range(chunks):
        a_copy(j).wait_send()
        sweep(first, j).wait_send()
        each(Z - 1, lambda k: d_copy(j, (z + 1 + k) % Z).wait_send())

        @pl.when(inner)
        def _():
            sweep(second, j).wait_send()

    for i in range(2):
        wx_copy(i).wait_send()
        wy_copy(i, dme).wait_send()
        wc_copy(i, dme, 0).wait_send()
        wc_copy(i, across, 1).wait_send()

    def ends(j):
        for copy in w_copies(j) + e_copies(j):
            copy.wait_send()

    each(n - 1, ends)
    for j in range(1, ndp):
        src = (dme + ndp - j) % ndp
        remote(q_send, q_recv.at[src], q_ss.at[j], q_rs.at[src], dp=dme).wait_recv()
        grad = grad + q_recv[src]
        q_copy(j).wait_send()
    grad_out[...] = grad


def on_device(
    n, ndp, table, triples, words, labels, in_gain, up_weight, down_weight, out_gain, class_weight
):
    ids = jnp.concatenate([triples, words], axis=1)
    seq = ids.shape[1]
    rows = ids.size
    tok = rows // n
    entries, width = table.shape
    units = up_weight.shape[1]
    feat = width // n
    Z = n // 2
    T = triples.shape[0]
    dma = pltpu.SemaphoreType.DMA
    vm = pl.BlockSpec(memory_space=pltpu.VMEM)
    hbm = pl.BlockSpec(memory_space=pl.ANY)
    r = min(tok, 16)
    CH = tok // r
    CR = Z * r
    ids = ids.reshape(Z, 2, CH, r).transpose(1, 2, 0, 3).reshape(2, Z * tok, 1)
    blk = pltpu.VMEM((CH, CR, width), BF16)
    wide = max(128, feat)
    enc, scores, grad = pl.pallas_call(
        functools.partial(kernel, n, ndp, seq),
        out_shape=(
            jax.ShapeDtypeStruct((n, tok, feat), BF16),
            jax.ShapeDtypeStruct((1, T), F32),
            jax.ShapeDtypeStruct((1, feat), F32),
        ),
        in_specs=[vm, hbm, hbm, hbm, vm, vm, vm, pl.BlockSpec(memory_space=pltpu.SMEM)],
        out_specs=(vm, vm, vm),
        scratch_shapes=[
            pltpu.VMEM((entries, width), BF16),
            pltpu.VMEM((width, units), BF16),
            pltpu.VMEM((units, width), BF16),
            pltpu.VMEM((width, units), BF16),
            pltpu.VMEM((units, width), BF16),
            blk, blk, blk,
            pltpu.VMEM((2, CH, CR, width), BF16),
            pltpu.VMEM((2, CH, CR, width), BF16),
            pltpu.VMEM((Z, r, width), BF16),
            pltpu.VMEM((Z, r, width), F32),
            pltpu.VMEM((CH, r, width), F32),
            pltpu.VMEM((CH, r, width), F32),
            pltpu.VMEM((CH, Z, r, width), BF16),
            pltpu.VMEM((CH, Z, r, width), BF16),
            pltpu.VMEM((n, 1, feat), F32),
            pltpu.VMEM((n, 1, feat), F32),
            pltpu.VMEM((n, tok, feat), BF16),
            pltpu.VMEM((n, tok, feat), BF16),
            pltpu.VMEM((8, wide), F32),
            pltpu.VMEM((n, 8, wide), F32),
            pltpu.VMEM((1, feat), F32),
            pltpu.VMEM((ndp, 1, feat), F32),
            dma((3,)),
            dma((2,)), dma((2,)), dma((2,)), dma((2,)), dma((2, 2)), dma((2, 2)),
            dma((CH,)), dma((CH,)), dma((2, CH)), dma((2, CH)), dma((CH, Z)), dma((CH, Z)),
            dma((2, n)), dma((2, n)),
            dma((n,)), dma((n,)), dma((n,)), dma((n,)),
            dma((ndp,)), dma((ndp,)),
        ],
        compiler_params=pltpu.CompilerParams(
            collective_id=0, has_side_effects=True, vmem_limit_bytes=63 * 1024 * 1024
        ),
    )(
        ids, table, up_weight, down_weight, in_gain.reshape(1, -1),
        out_gain.reshape(1, -1), class_weight.reshape(1, -1), labels,
    )
    return enc.reshape(rows, feat), scores.reshape(-1), grad.reshape(-1)


def solution(mesh):
    return jax.shard_map(
        functools.partial(on_device, mesh.shape["mp"], mesh.shape["dp"]),
        mesh=mesh,
        in_specs=(
            P("mp", None), P("dp", None), P("dp", None), P("dp"), P(),
            P(None, "mp"), P("mp", None), P("mp"), P("mp"),
        ),
        out_specs=(P("dp", "mp"), P("dp"), P("mp")),
        check_vma=False,
    )
```

time: 81.2 us -> 78.8 us (0.970)
  local copies, waits for them, and re-layouts: 7.69 us -> 5.59 us
    unnamed x16 -> x4, local copies, waits for them, and re-layouts: 7.54 us -> 4.64 us
where the time goes in v2:
time: 78.8 us; the launch traced here: 78.6 us
  Pallas kernels  71.6 us (91%)
  local copies, waits for them, and re-layouts  5.59 us (7%)
    pallas_call x1, Pallas kernels, on_device(): pl.pallas_call(functools.partial(kernel, n, ndp, seq), out_shape=(jax.Sha...  71.6 us
    unnamed x4, local copies, waits for them, and re-layouts  4.64 us

profile of v2, /device:TPU:0, one launch (start us, length us, event | category | flops | bytes accessed | tf_op | source)
XLA Modules:
  0.0 78.6 jit_solution(13030017167621843824)
XLA Ops:
  0.6 0.8 copy.14
  1.4 0.8 pad_add_fusion
  2.1 0.1 reshape.30
  2.2 0.9 %reshape.38.ids = s32[2,256,1]{2,1,0:T(8,128)} reshape(s32[2,4,4,16]{3,2,1,0:T(4,128)S(1)} %bitcast.10) | data formatting | bytes 4096 | tf_op jit(solution)/shard_map/reshape | solution.py:337
  3.1 71.6 %shard_map.112 = (bf16[8,64,128]{2,1,0:T(8,128)(2,1)}, f32[1,8]{1,0:T(1,128)}, f32[1,128]{1,0:T(1,128)}) custom-call(s32[2,256,1]{2,1,0:T(8,128)} %reshape.38.ids, bf16[2048,1024]{1,0:T(8,128)(2,1)} %table.1, bf16[1024,512]{1,0:T(8,128)(2,1)} %up.1, bf16[512,1024]{1,0:T(8,128)(2,1)} %down.1, f32[1,1024]{1,0:T(1,128)} %bitcast.11, f32[1,128]{1,0:T(1,128)} %bitcast.12, ...), custom_call_target="tpu_custom_call" | custom-call | tf_op jit(solution)/shard_map/pallas_call | solution.py:340
  74.7 1.6 %copy.22 = bf16[512,128]{1,0:T(8,128)(2,1)} copy(bf16[512,128]{1,0:T(8,128)(2,1)} %bitcast.9) | data formatting | bytes 262144
  76.2 1.1 %copy.23 = f32[8]{0:T(128)} copy(f32[8]{0:T(128)} %bitcast.15) | data formatting | bytes 64
  77.4 1.2 %copy.24 = f32[128]{0:T(128)} copy(f32[128]{0:T(128)} %bitcast.14) | data formatting | bytes 1024
  (1 shorter events, 0.0 us)

commit v3 on v2

--- a/solution.py
+++ b/solution.py
@@ -93,8 +93,6 @@
         ref = pairs[i][1]
         return remote(quarter(ref, d), quarter(ref, d), wc_ss.at[i, k], wc_rs.at[i, k], dp=beside)
 
-    wx_copy(0).start()
-    wx_copy(1).start()
 
     def w_copies(j):
         p = (me + 1 + j) % n
@@ -126,14 +124,12 @@
     for j in range(chunks):
         a_send[j] = rows[j * chunk_rows:(j + 1) * chunk_rows]
         a_copy(j).start()
+    wx_copy(0).start()
+    wx_copy(1).start()
     rows = half(x)
     for j in range(chunks):
         own[j] = rows[j * chunk_rows:(j + 1) * chunk_rows]
 
-    for i in range(2):
-        wx_copy(i).wait_recv()
-        wy_copy(i, dme).start()
-        wc_copy(i, dme, 0).start()
 
     first = z // (Z // 2)
     second = 1 - first
@@ -174,7 +170,7 @@
     def act(hidden):
         return (0.5 * hidden * (1.0 + lax.erf(hidden * (1.0 / math.sqrt(2.0))))).astype(BF16)
 
-    def finish(j):
+    def pass_back(j):
         sweep_in(second, j).wait_recv()
 
         @pl.when(inner)
@@ -182,16 +178,11 @@
             sw_send[second, j] = own[j] + sw_recv[second, j]
             sweep(second, j).start()
 
+    def finish(j):
         full = own[j] + sw_recv[0, j] + sw_recv[1, j]
         for zk in range(Z):
             rows_v[zk] = full[zk * r:(zk + 1) * r]
         keep[j] = rows_v[z].astype(F32)
-        if j == 0:
-            for i in range(2):
-                wc_copy(i, beside, 0).wait_recv()
-                wc_copy(i, (beside + ndp // 2) % ndp, 1).wait_recv()
-            loads[1].wait()
-            loads[2].wait()
         mine = act(jnp.dot(full, up_v[...], preferred_element_type=F32))
         theirs = act(jnp.dot(full, upx_v[...], preferred_element_type=F32))
         terms = jnp.dot(mine, down_v[...], preferred_element_type=F32)
@@ -202,16 +193,38 @@
         each(Z - 1, lambda k: d_copy(j, (z + 1 + k) % Z).start())
         part[j] = terms_v[z]
 
-    lag = min(2, chunks)
+    def relay(i):
+        wx_copy(i).wait_recv()
+        wy_copy(i, dme).start()
+        wc_copy(i, dme, 0).start()
+
+    def relay_on(i):
+        wy_copy(i, across).wait_recv()
+        wc_copy(i, across, 1).start()
+
+    early, lag = 0, min(2, chunks)
+    for i in range(early):
+        relay(i)
     for t in range(chunks + lag):
         if t < chunks:
             arrive(t)
         if t == 0:
-            for i in range(2):
-                wy_copy(i, across).wait_recv()
-                wc_copy(i, across, 1).start()
+            for i in range(early):
+                relay_on(i)
+        if t == chunks - 1:
+            for i in range(early, 2):
+                relay(i)
         if t >= lag:
-            finish(t - lag)
+            pass_back(t - lag)
+    for i in range(early, 2):
+        relay_on(i)
+    for i in range(2):
+        wc_copy(i, beside, 0).wait_recv()
+        wc_copy(i, (beside + ndp // 2) % ndp, 1).wait_recv()
+    loads[1].wait()
+    loads[2].wait()
+    for j in range(chunks):
+        finish(j)
 
     def w_in(j):
         src = (me + n - 1 - j) % n

time: 78.8 us -> 73 us (0.926)
  Pallas kernels: 71.6 us -> 65.8 us
    pallas_call x1, Pallas kernels: 71.6 us -> 65.8 us  [on_device(): pl.pallas_call(functools.partial(kernel, n, ndp, seq), out_shape=(jax.Sha...]
where the time goes in v3:
time: 73 us; the launch traced here: 72.8 us
  Pallas kernels  65.8 us (90%)
  local copies, waits for them, and re-layouts  5.59 us (8%)
  other arithmetic  0.76 us (1%)
    pallas_call x1, Pallas kernels, on_device(): pl.pallas_call(functools.partial(kernel, n, ndp, seq), out_shape=(jax.Sha...  65.8 us
    unnamed x4, local copies, waits for them, and re-layouts  4.64 us

profile of v3, /device:TPU:0, one launch (start us, length us, event | category | flops | bytes accessed | tf_op | source)
XLA Modules:
  0.0 72.8 jit_solution(13369713065938065445)
XLA Ops:
  0.6 0.8 %copy.14 = s32[8,3]{1,0:T(8,128)S(1)} copy(s32[8,3]{0,1:T(4,128)} %param.10) | data formatting | bytes 192 | tf_op args[1]
  1.4 0.8 %pad_add_fusion = s32[8,64]{1,0:T(8,128)S(1)} fusion(s32[8,61]{1,0:T(8,128)} %param.11, s32[8,3]{1,0:T(8,128)S(1)} %copy.14), kind=kLoop, calls=%fused_computation.1 | loop fusion | flops 512 | bytes 4096 | tf_op jit(solution)/shard_map/concatenate | solution.py:335
  2.1 0.1 reshape.30
  2.2 0.9 %reshape.38.ids = s32[2,256,1]{2,1,0:T(8,128)} reshape(s32[2,4,4,16]{3,2,1,0:T(4,128)S(1)} %bitcast.10) | data formatting | bytes 4096 | tf_op jit(solution)/shard_map/reshape | solution.py:350
  3.1 65.8 %shard_map.112 = (bf16[8,64,128]{2,1,0:T(8,128)(2,1)}, f32[1,8]{1,0:T(1,128)}, f32[1,128]{1,0:T(1,128)}) custom-call(s32[2,256,1]{2,1,0:T(8,128)} %reshape.38.ids, bf16[2048,1024]{1,0:T(8,128)(2,1)} %table.1, bf16[1024,512]{1,0:T(8,128)(2,1)} %up.1, bf16[512,1024]{1,0:T(8,128)(2,1)} %down.1, f32[1,1024]{1,0:T(1,128)} %bitcast.11, f32[1,128]{1,0:T(1,128)} %bitcast.12, ...), custom_call_target="tpu_custom_call" | custom-call | tf_op jit(solution)/shard_map/pallas_call | solution.py:353
  68.9 1.6 %copy.22 = bf16[512,128]{1,0:T(8,128)(2,1)} copy(bf16[512,128]{1,0:T(8,128)(2,1)} %bitcast.9) | data formatting | bytes 262144
  70.4 1.1 %copy.23 = f32[8]{0:T(128)} copy(f32[8]{0:T(128)} %bitcast.15) | data formatting | bytes 64
  71.6 1.2 %copy.24 = f32[128]{0:T(128)} copy(f32[128]{0:T(128)} %bitcast.14) | data formatting | bytes 1024
  (1 shorter events, 0.0 us)
